TPU v7x, 32 devices: a whole 2x2x4 slice. The times are simulated.
32 devices in a mesh: src: 4 (over y, x), blk: 8 (over z, core).
Axes of the slice: x: 2, y: 2, z: 4, core: 2. Of those that a mesh axis runs over, the one named last changes fastest.
Arguments:
- values: float32 [4, 512, 32, 128], P('src', 'blk'), may hold values from -0.25 to 0.25
- diagonal: float32 [4, 512, 128], P('src', 'blk'), may hold values from 0.55 to 0.95
- rhs_parts: float32 [4, 512, 128], P('src', 'blk'), may hold values from -24 to 24
- owner_map: int32 [512, 128], P('blk'), may hold values from 0 to 3
- columns: int32 [512, 32, 128], P('blk'), may hold values from 0 to 1073741823
- destination: int32 [512, 1], P('blk'), may hold values from 0 to 7; in each aligned block of 64 rows (0 to 63, 64 to 127, ...) at most 16 rows name the same one
- order_keys: int32 [512], P('blk'), may hold values from 0 to 511, each once
Outputs:
- solution: float32 [512, 128], P('blk')
Inputs may be any that keep to these rules, and one draw needn't show every extreme that they name: `destination`: among the row blocks of one index of blk no owner is named more than 16 times, some owner is named exactly 16 times, and every owner is named by some block. `order_keys`: each key appears once.
All inputs are finite; a program needn't handle non-finite values.
Results may differ from a plain program's by a relative error of at most 0.0003.
Values sent between devices are 32-bit elements; how exact they have to be, the bound alone decides.
No kernel may reach another device: no remote copies, remote signals or barrier semaphores. Data moves between devices by JAX's collectives and lax.ppermute only.
A program may use at most 64 MiB of HBM per device.

v0:
```python
import jax
import jax.numpy as jnp
from jax import lax
from jax.sharding import PartitionSpec as P

SWEEPS = 3


def tile_matrix(block_vals, block_cols, tile_rows):
    slot_count = block_vals.shape[0]
    stored = block_vals.shape[1]
    groups = 8
    lanes = jnp.remainder(block_cols, 2 * tile_rows)
    targets = jnp.arange(2 * tile_rows, dtype=jnp.int32)
    grouped_vals = block_vals.reshape(groups, slot_count // groups, stored, tile_rows)
    grouped_lanes = lanes.reshape(groups, slot_count // groups, stored, tile_rows)

    def build(pair):
        group_vals, group_lanes = pair
        picked = jnp.where(group_lanes[..., None] == targets, group_vals[..., None], 0.0)
        return jnp.sum(picked, axis=1)

    dense = lax.map(build, (grouped_vals, grouped_lanes))
    return dense.reshape(slot_count, tile_rows, 2 * tile_rows)


def on_device(values, diagonal, rhs_parts, owner_map, columns, destination, order_keys):
    owners = lax.axis_size("blk")
    part_count = lax.axis_size("src")
    tile_count = destination.shape[0]
    stored = values.shape[2]
    tile_rows = values.shape[3]
    per_peer = 2 * tile_count // owners
    slot_count = owners * per_peer
    owner_of = destination[:, 0]
    tile_ids = jnp.arange(tile_count, dtype=jnp.int32)
    slot_ids = jnp.arange(slot_count, dtype=jnp.int32)
    earlier = (owner_of[None, :] == owner_of[:, None]) & (tile_ids[None, :] < tile_ids[:, None])
    position = jnp.sum(earlier, axis=1)
    slot_of = owner_of * per_peer + position
    slot_hits = slot_of[None, :] == slot_ids[:, None]
    filled = jnp.any(slot_hits, axis=1)
    source_tile = jnp.sum(jnp.where(slot_hits, tile_ids[None, :], 0), axis=1)
    is_owned = owner_map == lax.axis_index("src")
    own_rhs = jnp.where(is_owned, rhs_parts[0], 0.0)
    send_vals = jnp.where(filled[:, None, None], values[0][source_tile], 0.0)
    send_diag = jnp.where(filled[:, None], diagonal[0][source_tile], 0.0)
    send_rhs = jnp.where(filled[:, None], own_rhs[source_tile], 0.0)
    send_cols = columns[source_tile]
    send_keys = jnp.where(filled, order_keys[source_tile], -1)
    quarter = stored // part_count
    part_vals = lax.psum_scatter(send_vals, "src", scatter_dimension=1, tiled=True)
    sum_diag, sum_rhs = lax.psum((send_diag, send_rhs), "src")
    part_cols = lax.dynamic_slice_in_dim(send_cols, lax.axis_index("src") * quarter, quarter, 1)
    got_vals, got_diag, got_rhs = (
        lax.all_to_all(part_vals, "blk", split_axis=0, concat_axis=0, tiled=True),
        lax.all_to_all(sum_diag, "blk", split_axis=0, concat_axis=0, tiled=True),
        lax.all_to_all(sum_rhs, "blk", split_axis=0, concat_axis=0, tiled=True),
    )
    got_cols, got_keys = (
        lax.all_to_all(part_cols, "blk", split_axis=0, concat_axis=0, tiled=True),
        lax.all_to_all(send_keys, "blk", split_axis=0, concat_axis=0, tiled=True),
    )
    is_live = got_keys >= 0
    tile_total = jnp.sum(is_live)
    smaller = is_live[None, :] & (got_keys[None, :] < got_keys[:, None])
    tile_rank = jnp.sum(smaller, axis=1)
    rank_hits = is_live[None, :] & (tile_rank[None, :] == slot_ids[:, None])
    holder = jnp.sum(jnp.where(rank_hits, slot_ids[None, :], 0), axis=1)
    occupied = slot_ids < tile_total
    block_vals = jnp.where(occupied[:, None, None], got_vals[holder], 0.0)
    block_cols = got_cols[holder]
    right_side = jnp.where(occupied[:, None], got_rhs[holder], 0.0)
    block_diag = jnp.where(occupied[:, None], got_diag[holder], 1.0)
    dense = tile_matrix(block_vals, block_cols, tile_rows)
    following = jnp.remainder(slot_ids + 1, tile_total)
    iterate = jnp.zeros((slot_count, tile_rows), jnp.float32)
    for sweep_index in range(SWEEPS):
        nearby = jnp.concatenate([iterate, iterate[following]], axis=1)
        partial_sum = jnp.sum(dense * nearby[:, None, :], axis=2)
        summed = lax.psum(partial_sum, "src")
        iterate = jnp.where(occupied[:, None], (right_side - summed) / block_diag, 0.0)
    in_slots = jnp.where(is_live[:, None], iterate[tile_rank], 0.0)
    returned = lax.all_to_all(in_slots, "blk", split_axis=0, concat_axis=0, tiled=True)
    return returned[slot_of]


def solution(mesh):
    placed = (
        P("src", "blk", None, None),
        P("src", "blk", None),
        P("src", "blk", None),
        P("blk", None),
        P("blk", None, None),
        P("blk", None),
        P("blk"),
    )
    return jax.shard_map(
        on_device, mesh=mesh, in_specs=placed, out_specs=P("blk", None), check_vma=False
    )
```

profile of v0, /device:TPU:0, one launch (start us, length us, event | category | flops | bytes accessed | tf_op | source)
XLA Modules:
  0.0 320.4 jit_solution(3956767261336183481)
XLA Ops:
  6.6 0.9 convert_reduce_fusion.1
  8.4 0.8 gather_fusion.5
  9.2 1.6 broadcast_select_fusion
  10.8 1.6 gather_fusion
  13.1 6.4 %all-to-all-start = ((s32[8,16,1]{1,2,0:T(1,128)}), s32[8,16,1]{1,2,0:T(1,128)S(1)}, u32[]{:S(2)}, u32[]{:S(2)}) async-start(s32[8,16,1]{1,2,0:T(1,128)} %bitcast.3), calls=%async_computation | async-start | bytes 8192 | tf_op jit(solution)/shard_map/all_to_all | solution.py:62
  19.4 2.2 gather_fusion.3
  21.6 0.9 constant_dynamic-slice_fusion
  22.5 2.4 all-to-all-done
  24.9 3.5 %all-to-all-start.2 = ((s32[128,8,128]{2,1,0:T(8,128)}), s32[128,8,128]{2,1,0:T(8,128)S(1)}, u32[]{:S(2)}, u32[]{:S(2)}) async-start(s32[128,8,128]{2,1,0:T(8,128)} %constant_dynamic-slice_fusion), calls=%async_computation.2 | async-start | bytes 1048576 | tf_op jit(solution)/shard_map/all_to_all | solution.py:61
  29.8 0.7 broadcast_select_fusion.4
  34.5 9.2 %all-to-all-done.2 = s32[128,8,128]{2,1,0:T(8,128)S(1)} async-done(((s32[128,8,128]{2,1,0:T(8,128)}), s32[128,8,128]{2,1,0:T(8,128)S(1)}, u32[]{:S(2)}, u32[]{:S(2)}) %all-to-all-start.2) | async-done | bytes 524320 | tf_op jit(solution)/shard_map/all_to_all | solution.py:61
  43.7 5.2 %reduce-scatter.2.cloned.1.call-done = f32[128,8,128]{2,1,0:T(8,128)} async-done(((f32[128,32,128]{2,1,0:T(8,128)}), f32[128,8,128]{2,1,0:T(8,128)}) %reduce-scatter.2.cloned.1.call-update) | async-done | bytes 524304 | tf_op jit(solution)/shard_map/reduce_scatter | solution.py:52
  48.9 4.6 %all-to-all-start.3 = ((f32[128,8,128]{2,1,0:T(8,128)}), f32[128,8,128]{2,1,0:T(8,128)S(1)}, u32[]{:S(2)}, u32[]{:S(2)}) async-start(f32[128,8,128]{2,1,0:T(8,128)} %reduce-scatter.2.cloned.1.call-done), calls=%async_computation.4 | async-start | bytes 1048576 | tf_op jit(solution)/shard_map/all_to_all | solution.py:56
  54.5 0.8 gather_fusion.4
  55.5 13.3 %all-to-all-done.3 = f32[128,8,128]{2,1,0:T(8,128)S(1)} async-done(((f32[128,8,128]{2,1,0:T(8,128)}), f32[128,8,128]{2,1,0:T(8,128)S(1)}, u32[]{:S(2)}, u32[]{:S(2)}) %all-to-all-start.3) | async-done | bytes 524320 | tf_op jit(solution)/shard_map/all_to_all | solution.py:56
  68.8 0.8 gather_fusion.6
  69.8 57.8 %while.11 = (s32[]{:T(128)}, f32[8,16,128,256]{3,2,1,0:T(8,128)}, s32[8,16,8,128]{3,2,1,0:T(8,128)S(1)}, f32[8,16,8,128]{3,2,1,0:T(8,128)S(1)}, s32[]{:T(128)}) while((s32[]{:T(128)}, f32[8,16,128,256]{3,2,1,0:T(8,128)}, s32[8,16,8,128]{3,2,1,0:T(8,128)S(1)}, f32[8,16,8,128]{3,2,1,0:T(8,128)S(1)}, s32[]{:T(128)}) %tuple.23), condition=%wide.region_10.11_spmd.clone, body=%wide.region_8.10_spmd.clone.sunk | while | flops 12058626 | bytes 6685253 | solution.py:23
  69.8 5.7 %select_reduce_fusion.4 = f32[16,128,256]{2,1,0:T(8,128)S(1)} fusion(f32[16,8,128]{2,1,0:T(8,128)S(1)} %dynamic-slice_bitcast_fusion.4, s32[16,8,128]{2,1,0:T(8,128)S(1)} %dynamic-slice_bitcast_fusion.5), kind=kLoop, calls=%fused_computation.16.clone.1 | loop fusion | flops 12058624 | bytes 2228224 | tf_op jit(solution)/shard_map/while/body/eval_jaxpr/reduce_sum | solution.py:21
  75.5 1.6 bitcast_dynamic-update-slice_fusion.2
  77.1 5.7 %select_reduce_fusion.4 = f32[16,128,256]{2,1,0:T(8,128)S(1)} fusion(f32[16,8,128]{2,1,0:T(8,128)S(1)} %dynamic-slice_bitcast_fusion.4, s32[16,8,128]{2,1,0:T(8,128)S(1)} %dynamic-slice_bitcast_fusion.5), kind=kLoop, calls=%fused_computation.16.clone.1 | loop fusion | flops 12058624 | bytes 2228224 | tf_op jit(solution)/shard_map/while/body/eval_jaxpr/reduce_sum | solution.py:21
  82.7 1.5 bitcast_dynamic-update-slice_fusion.2
  84.2 5.7 %select_reduce_fusion.4 = f32[16,128,256]{2,1,0:T(8,128)S(1)} fusion(f32[16,8,128]{2,1,0:T(8,128)S(1)} %dynamic-slice_bitcast_fusion.4, s32[16,8,128]{2,1,0:T(8,128)S(1)} %dynamic-slice_bitcast_fusion.5), kind=kLoop, calls=%fused_computation.16.clone.1 | loop fusion | flops 12058624 | bytes 2228224 | tf_op jit(solution)/shard_map/while/body/eval_jaxpr/reduce_sum | solution.py:21
  89.9 1.5 bitcast_dynamic-update-slice_fusion.2
  91.5 5.7 %select_reduce_fusion.4 = f32[16,128,256]{2,1,0:T(8,128)S(1)} fusion(f32[16,8,128]{2,1,0:T(8,128)S(1)} %dynamic-slice_bitcast_fusion.4, s32[16,8,128]{2,1,0:T(8,128)S(1)} %dynamic-slice_bitcast_fusion.5), kind=kLoop, calls=%fused_computation.16.clone.1 | loop fusion | flops 12058624 | bytes 2228224 | tf_op jit(solution)/shard_map/while/body/eval_jaxpr/reduce_sum | solution.py:21
  97.1 1.5 bitcast_dynamic-update-slice_fusion.2
  98.7 5.7 %select_reduce_fusion.4 = f32[16,128,256]{2,1,0:T(8,128)S(1)} fusion(f32[16,8,128]{2,1,0:T(8,128)S(1)} %dynamic-slice_bitcast_fusion.4, s32[16,8,128]{2,1,0:T(8,128)S(1)} %dynamic-slice_bitcast_fusion.5), kind=kLoop, calls=%fused_computation.16.clone.1 | loop fusion | flops 12058624 | bytes 2228224 | tf_op jit(solution)/shard_map/while/body/eval_jaxpr/reduce_sum | solution.py:21
  104.4 1.6 bitcast_dynamic-update-slice_fusion.2
  106.0 5.7 %select_reduce_fusion.4 = f32[16,128,256]{2,1,0:T(8,128)S(1)} fusion(f32[16,8,128]{2,1,0:T(8,128)S(1)} %dynamic-slice_bitcast_fusion.4, s32[16,8,128]{2,1,0:T(8,128)S(1)} %dynamic-slice_bitcast_fusion.5), kind=kLoop, calls=%fused_computation.16.clone.1 | loop fusion | flops 12058624 | bytes 2228224 | tf_op jit(solution)/shard_map/while/body/eval_jaxpr/reduce_sum | solution.py:21
  111.6 1.5 bitcast_dynamic-update-slice_fusion.2
  113.1 5.7 %select_reduce_fusion.4 = f32[16,128,256]{2,1,0:T(8,128)S(1)} fusion(f32[16,8,128]{2,1,0:T(8,128)S(1)} %dynamic-slice_bitcast_fusion.4, s32[16,8,128]{2,1,0:T(8,128)S(1)} %dynamic-slice_bitcast_fusion.5), kind=kLoop, calls=%fused_computation.16.clone.1 | loop fusion | flops 12058624 | bytes 2228224 | tf_op jit(solution)/shard_map/while/body/eval_jaxpr/reduce_sum | solution.py:21
  118.8 1.6 bitcast_dynamic-update-slice_fusion.2
  120.4 5.7 %select_reduce_fusion.4 = f32[16,128,256]{2,1,0:T(8,128)S(1)} fusion(f32[16,8,128]{2,1,0:T(8,128)S(1)} %dynamic-slice_bitcast_fusion.4, s32[16,8,128]{2,1,0:T(8,128)S(1)} %dynamic-slice_bitcast_fusion.5), kind=kLoop, calls=%fused_computation.16.clone.1 | loop fusion | flops 12058624 | bytes 2228224 | tf_op jit(solution)/shard_map/while/body/eval_jaxpr/reduce_sum | solution.py:21
  126.1 1.5 bitcast_dynamic-update-slice_fusion.2
  127.6 8.6 %multiply_reduce_fusion.2 = f32[8,16,128]{2,1,0:T(8,128)} fusion(f32[8,16,128,256]{3,2,1,0:T(8,128)} %get-tuple-element.32, f32[8,16,256]{2,1,0:T(8,128)S(1)} %bitcast.63), kind=kLoop, calls=%fused_computation.22 | loop fusion | flops 8372224 | bytes 16973824 | tf_op jit(solution)/shard_map/reduce_sum | solution.py:80
  136.2 41.3 %all-reduce.10.cloned.1.call-done = (f32[128,128]{1,0:T(8,128)}, f32[8,16,128]{2,1,0:T(8,128)}, f32[8,16,128]{2,1,0:T(8,128)}) async-done(((f32[128,128]{1,0:T(8,128)}, f32[8,16,128]{2,1,0:T(8,128)}, f32[8,16,128]{2,1,0:T(8,128)}), (f32[128,128]{1,0:T(8,128)}, f32[8,16,128]{2,1,0:T(8,128)}, f32[8,16,128]{2,1,0:T(8,128)})) %all-reduce.10.cloned.1.call-update) | async-done | bytes 196624 | tf_op jit(solution)/shard_map/psum | solution.py:81
  177.5 10.5 %all_to_all.52 = f32[8,16,128]{2,1,0:T(8,128)S(1)} all-to-all(f32[8,16,128]{2,1,0:T(8,128)} %get-tuple-element.53), channel_id=1, replica_groups=mesh['src'=4,'blk'=8] {'blk'}, dimensions={0} | all-to-all | bytes 131072 | tf_op jit(solution)/shard_map/all_to_all | solution.py:58
  188.0 3.3 %all-to-all-start.4 = ((f32[8,16,128]{2,1,0:T(8,128)}), f32[8,16,128]{2,1,0:T(8,128)S(1)}, u32[]{:S(2)}, u32[]{:S(2)}) async-start(f32[8,16,128]{2,1,0:T(8,128)} %get-tuple-element.52), calls=%async_computation.5 | async-start | bytes 131072 | tf_op jit(solution)/shard_map/all_to_all | solution.py:57
  192.7 4.5 %all-to-all-done.4 = f32[8,16,128]{2,1,0:T(8,128)S(1)} async-done(((f32[8,16,128]{2,1,0:T(8,128)}), f32[8,16,128]{2,1,0:T(8,128)S(1)}, u32[]{:S(2)}, u32[]{:S(2)}) %all-to-all-start.4) | async-done | bytes 65568 | tf_op jit(solution)/shard_map/all_to_all | solution.py:57
  197.9 0.9 divide_select_fusion.2
  199.5 8.6 %multiply_reduce_fusion.1 = f32[8,16,128]{2,1,0:T(8,128)} fusion(f32[8,16,128,256]{3,2,1,0:T(8,128)} %get-tuple-element.32, f32[8,16,256]{2,1,0:T(8,128)S(1)} %bitcast.65), kind=kLoop, calls=%fused_computation.21 | loop fusion | flops 8372224 | bytes 16973824 | tf_op jit(solution)/shard_map/reduce_sum | solution.py:80
  208.4 39.3 %all-reduce.6.cloned.1.call-done = f32[128,128]{1,0:T(8,128)} async-done(((f32[128,128]{1,0:T(8,128)}), f32[128,128]{1,0:T(8,128)}) %all-reduce.6.cloned.1.call-update) | async-done | bytes 65552 | tf_op jit(solution)/shard_map/psum | solution.py:81
  247.6 0.9 divide_select_fusion.1
  249.2 8.6 %multiply_reduce_fusion = f32[8,16,128]{2,1,0:T(8,128)} fusion(f32[8,16,128,256]{3,2,1,0:T(8,128)} %get-tuple-element.32, f32[8,16,256]{2,1,0:T(8,128)S(1)} %bitcast.64), kind=kLoop, calls=%fused_computation.20 | loop fusion | flops 8372224 | bytes 16973824 | tf_op jit(solution)/shard_map/reduce_sum | solution.py:80
  257.9 42.0 %all-reduce.8.cloned.1.call-done = f32[128,128]{1,0:T(8,128)} async-done(((f32[128,128]{1,0:T(8,128)}), f32[128,128]{1,0:T(8,128)}) %all-reduce.8.cloned.1.call-update) | async-done | bytes 65552 | tf_op jit(solution)/shard_map/psum | solution.py:81
  299.9 0.9 divide_select_fusion
  302.2 4.6 %all-to-all-start.5 = ((f32[8,16,128]{2,1,0:T(8,128)}), f32[8,16,128]{2,1,0:T(8,128)S(1)}, u32[]{:S(2)}, u32[]{:S(2)}) async-start(f32[8,16,128]{2,1,0:T(8,128)} %broadcast_select_fusion.2), calls=%async_computation.6 | async-start | bytes 131072 | tf_op jit(solution)/shard_map/all_to_all | solution.py:84
  306.8 5.9 %all-to-all-done.5 = f32[8,16,128]{2,1,0:T(8,128)S(1)} async-done(((f32[8,16,128]{2,1,0:T(8,128)}), f32[8,16,128]{2,1,0:T(8,128)S(1)}, u32[]{:S(2)}, u32[]{:S(2)}) %all-to-all-start.5) | async-done | bytes 65568 | tf_op jit(solution)/shard_map/all_to_all | solution.py:84
  312.7 1.2 gather_fusion.13
  (75 shorter events, 12.0 us)
Async XLA Ops:
  6.5 1.9 copy-start
  6.5 21.9 %copy-start.2 = (f32[1,64,128]{2,1,0:T(8,128)S(1)}, f32[1,64,128]{2,1,0:T(8,128)}, u32[]{:S(2)}) copy-start(f32[1,64,128]{2,1,0:T(8,128)} %param.11) | copy-start | bytes 98308
  6.5 21.9 %copy-start.3 = (s32[64,128]{1,0:T(8,128)S(1)}, s32[64,128]{1,0:T(8,128)}, u32[]{:S(2)}) copy-start(s32[64,128]{1,0:T(8,128)} %param.12) | copy-start | bytes 98308
  6.5 22.6 %copy-start.1 = (f32[1,64,128]{2,1,0:T(8,128)S(1)}, f32[1,64,128]{2,1,0:T(8,128)}, u32[]{:S(2)}) copy-start(f32[1,64,128]{2,1,0:T(8,128)} %param.10) | copy-start | bytes 98308
  6.5 42.3 %reduce-scatter.2.cloned.1.call-start = ((), (), s32[]{:S(2)}) async-start(), calls=%async_computation.7 | async-start | bytes 2621440 | tf_op jit(solution)/shard_map/reduce_scatter | solution.py:52
  13.1 11.9 %all-to-all-start = ((s32[8,16,1]{1,2,0:T(1,128)}), s32[8,16,1]{1,2,0:T(1,128)S(1)}, u32[]{:S(2)}, u32[]{:S(2)}) async-start(s32[8,16,1]{1,2,0:T(1,128)} %bitcast.3), calls=%async_computation | async-start | bytes 8192 | tf_op jit(solution)/shard_map/all_to_all | solution.py:62
  24.9 18.8 %all-to-all-start.2 = ((s32[128,8,128]{2,1,0:T(8,128)}), s32[128,8,128]{2,1,0:T(8,128)S(1)}, u32[]{:S(2)}, u32[]{:S(2)}) async-start(s32[128,8,128]{2,1,0:T(8,128)} %constant_dynamic-slice_fusion), calls=%async_computation.2 | async-start | bytes 1048576 | tf_op jit(solution)/shard_map/all_to_all | solution.py:61
  48.9 19.9 %all-to-all-start.3 = ((f32[128,8,128]{2,1,0:T(8,128)}), f32[128,8,128]{2,1,0:T(8,128)S(1)}, u32[]{:S(2)}, u32[]{:S(2)}) async-start(f32[128,8,128]{2,1,0:T(8,128)} %reduce-scatter.2.cloned.1.call-done), calls=%async_computation.4 | async-start | bytes 1048576 | tf_op jit(solution)/shard_map/all_to_all | solution.py:56
  53.5 124.0 %all-reduce.10.cloned.1.call-start = ((), (), s32[]{:S(2)}) async-start(), calls=%async_computation.10 | async-start | bytes 393216 | tf_op jit(solution)/shard_map/psum | solution.py:81
  188.0 9.2 %all-to-all-start.4 = ((f32[8,16,128]{2,1,0:T(8,128)}), f32[8,16,128]{2,1,0:T(8,128)S(1)}, u32[]{:S(2)}, u32[]{:S(2)}) async-start(f32[8,16,128]{2,1,0:T(8,128)} %get-tuple-element.52), calls=%async_computation.5 | async-start | bytes 131072 | tf_op jit(solution)/shard_map/all_to_all | solution.py:57
  191.4 56.3 %all-reduce.6.cloned.1.call-start = ((), (), s32[]{:S(2)}) async-start(), calls=%async_computation.8 | async-start | bytes 131072 | tf_op jit(solution)/shard_map/psum | solution.py:81
  199.5 107.3 %copy-start.4 = (s32[64,1]{0,1:T(1,128)S(1)}, s32[64,1]{0,1:T(1,128)}, u32[]{:S(2)}) copy-start(s32[64,1]{0,1:T(1,128)} %param.14) | copy-start | bytes 772
  208.1 91.7 %all-reduce.8.cloned.1.call-start = ((), (), s32[]{:S(2)}) async-start(), calls=%async_computation.9 | async-start | bytes 131072 | tf_op jit(solution)/shard_map/psum | solution.py:81
  302.2 10.5 %all-to-all-start.5 = ((f32[8,16,128]{2,1,0:T(8,128)}), f32[8,16,128]{2,1,0:T(8,128)S(1)}, u32[]{:S(2)}, u32[]{:S(2)}) async-start(f32[8,16,128]{2,1,0:T(8,128)} %broadcast_select_fusion.2), calls=%async_computation.6 | async-start | bytes 131072 | tf_op jit(solution)/shard_map/all_to_all | solution.py:84
Sparse Core Ops, SparseCore 0:
  10.9 37.9 reduce-scatter.1
  136.4 41.0 all-reduce.9
  208.2 39.3 all-reduce.5
  258.0 41.8 all-reduce.7
where the time goes:
time: 321 us; the launch traced here: 320 us
  waiting for transfers between devices  163 us (51%)
  other arithmetic  82.2 us (26%)
  local copies, waits for them, and re-layouts  27 us (8%)
  starting transfers between devices  22.7 us (7%)
  between operations  14.7 us (5%)
  blocking collectives  10.5 us (3%)
    psum x3, waiting for transfers between devices, on_device(): summed = lax.psum(partial_sum, 'src')  123 us
    reduce_sum x8, other arithmetic, build(): return jnp.sum(picked, axis=1)  45.3 us
    reduce_sum x3, other arithmetic, on_device(): partial_sum = jnp.sum(dense * nearby[:, None, :], axis=2)  25.9 us
    all_to_all x1, waiting for transfers between devices, on_device(): lax.all_to_all(part_vals, 'blk', split_axis=0, concat_axis=0, tiled=True)  13.3 us
    dynamic_update_slice x8, local copies, waits for them, and re-layouts, tile_matrix(): dense = lax.map(build, (grouped_vals, grouped_lanes))  12.3 us
    all_to_all x1, blocking collectives, on_device(): lax.all_to_all(sum_rhs, 'blk', split_axis=0, concat_axis=0, tiled=True)  10.5 us
    all_to_all x1, waiting for transfers between devices, on_device(): lax.all_to_all(part_cols, 'blk', split_axis=0, concat_axis=0, tiled=True)  9.16 us
  transfers between devices with their start and end apart: 9, of which 9 were waited for; matrix products, arithmetic and copies ran while one was open for 4% of the time, Pallas kernels for 0%

commit v1 on v0

--- a/solution.py
+++ b/solution.py
@@ -78,7 +78,7 @@
     for sweep_index in range(SWEEPS):
         nearby = jnp.concatenate([iterate, iterate[following]], axis=1)
         partial_sum = jnp.sum(dense * nearby[:, None, :], axis=2)
-        summed = lax.psum(partial_sum, "src")
+        summed = jnp.sum(lax.all_gather(partial_sum, "src"), axis=0)
         iterate = jnp.where(occupied[:, None], (right_side - summed) / block_diag, 0.0)
     in_slots = jnp.where(is_live[:, None], iterate[tile_rank], 0.0)
     returned = lax.all_to_all(in_slots, "blk", split_axis=0, concat_axis=0, tiled=True)

time: 321 us -> 246 us (0.77)
  waiting for transfers between devices: 163 us -> 67 us
  blocking collectives: 10.5 us -> 38 us
  starting transfers between devices: 22.7 us -> 19.1 us
  other arithmetic: 82.2 us -> 78.7 us
    psum x3 -> x1, waiting for transfers between devices: 123 us -> 29.3 us  [on_device(): sum_diag, sum_rhs = lax.psum((send_diag, send_rhs), 'src')]
    all_gather x0 -> x3, blocking collectives: none -> 26.3 us  [on_device(): summed = jnp.sum(lax.all_gather(partial_sum, 'src'), axis=0)]
    reduce_scatter x1, waiting for transfers between devices: 5.18 us -> 0.01 us  [on_device(): lax.psum_scatter(send_vals, 'src', scatter_dimension=1, tiled=True)]
  transfers between devices with their start and end apart: 9 -> 7, of which waited for: 9 -> 6; matrix products, arithmetic and copies ran while one was open for 4% -> 5% of each run, Pallas kernels for 0% -> 0%
where the time goes in v1:
time: 246 us; the launch traced here: 245 us
  other arithmetic  78.7 us (32%)
  waiting for transfers between devices  67 us (27%)
  blocking collectives  38 us (15%)
  local copies, waits for them, and re-layouts  26.9 us (11%)
  starting transfers between devices  19.1 us (8%)
  between operations  15 us (6%)
    reduce_sum x8, other arithmetic, build(): return jnp.sum(picked, axis=1)  45.3 us
    psum x1, waiting for transfers between devices, on_device(): sum_diag, sum_rhs = lax.psum((send_diag, send_rhs), 'src')  29.3 us
    all_gather x3, blocking collectives, on_device(): summed = jnp.sum(lax.all_gather(partial_sum, 'src'), axis=0)  26.3 us
    reduce_sum x3, other arithmetic, on_device(): partial_sum = jnp.sum(dense * nearby[:, None, :], axis=2)  24 us
    all_to_all x1, waiting for transfers between devices, on_device(): lax.all_to_all(part_vals, 'blk', split_axis=0, concat_axis=0, tiled=True)  13 us
    dynamic_update_slice x8, local copies, waits for them, and re-layouts, tile_matrix(): dense = lax.map(build, (grouped_vals, grouped_lanes))  12.3 us
    all_to_all x1, blocking collectives, on_device(): lax.all_to_all(send_keys, 'blk', split_axis=0, concat_axis=0, tiled=True)  11.7 us
    all_to_all x1, waiting for transfers between devices, on_device(): lax.all_to_all(part_cols, 'blk', split_axis=0, concat_axis=0, tiled=True)  9.86 us
  transfers between devices with their start and end apart: 7, of which 6 were waited for; matrix products, arithmetic and copies ran while one was open for 5% of the time, Pallas kernels for 0%

profile of v1, /device:TPU:0, one launch (start us, length us, event | category | flops | bytes accessed | tf_op | source)
XLA Modules:
  0.0 244.8 jit_solution(5694291346666444372)
XLA Ops:
  6.5 0.9 convert_reduce_fusion.1
  8.4 0.8 bitcast_select_fusion
  9.8 1.4 gather_fusion.8
  11.2 0.7 broadcast_select_fusion.4
  12.0 0.8 gather_fusion.5
  12.8 1.6 broadcast_select_fusion
  14.4 1.6 gather_fusion
  16.1 11.7 %all_to_all.52 = s32[8,16,1]{1,2,0:T(1,128)S(1)} all-to-all(s32[8,16,1]{1,2,0:T(1,128)S(1)} %bitcast.83), channel_id=1, replica_groups=mesh['src'=4,'blk'=8] {'blk'}, dimensions={0} | all-to-all | bytes 1024 | tf_op jit(solution)/shard_map/all_to_all | solution.py:62
  27.8 29.3 %all-reduce.4.cloned.1.call-done = (f32[8,16,128]{2,1,0:T(8,128)}, f32[8,16,128]{2,1,0:T(8,128)}) async-done(((f32[8,16,128]{2,1,0:T(8,128)}, f32[8,16,128]{2,1,0:T(8,128)}), (f32[8,16,128]{2,1,0:T(8,128)}, f32[8,16,128]{2,1,0:T(8,128)})) %all-reduce.4.cloned.1.call-update) | async-done | bytes 131088 | tf_op jit(solution)/shard_map/psum | solution.py:53
  57.1 4.6 %all-to-all-start.1 = ((f32[8,16,128]{2,1,0:T(8,128)}), f32[8,16,128]{2,1,0:T(8,128)S(1)}, u32[]{:S(2)}, u32[]{:S(2)}) async-start(f32[8,16,128]{2,1,0:T(8,128)} %get-tuple-element.52), calls=%async_computation.1 | async-start | bytes 131072 | tf_op jit(solution)/shard_map/all_to_all | solution.py:58
  61.7 1.9 gather_fusion.3
  63.6 4.0 %all-to-all-done.1 = f32[8,16,128]{2,1,0:T(8,128)S(1)} async-done(((f32[8,16,128]{2,1,0:T(8,128)}), f32[8,16,128]{2,1,0:T(8,128)S(1)}, u32[]{:S(2)}, u32[]{:S(2)}) %all-to-all-start.1) | async-done | bytes 65568 | tf_op jit(solution)/shard_map/all_to_all | solution.py:58
  67.6 3.3 %all-to-all-start.4 = ((f32[8,16,128]{2,1,0:T(8,128)}), f32[8,16,128]{2,1,0:T(8,128)S(1)}, u32[]{:S(2)}, u32[]{:S(2)}) async-start(f32[8,16,128]{2,1,0:T(8,128)} %get-tuple-element.51), calls=%async_computation.5 | async-start | bytes 131072 | tf_op jit(solution)/shard_map/all_to_all | solution.py:57
  71.0 0.9 constant_dynamic-slice_fusion
  71.9 5.0 %all-to-all-done.4 = f32[8,16,128]{2,1,0:T(8,128)S(1)} async-done(((f32[8,16,128]{2,1,0:T(8,128)}), f32[8,16,128]{2,1,0:T(8,128)S(1)}, u32[]{:S(2)}, u32[]{:S(2)}) %all-to-all-start.4) | async-done | bytes 65568 | tf_op jit(solution)/shard_map/all_to_all | solution.py:57
  76.8 3.5 %all-to-all-start.2 = ((s32[128,8,128]{2,1,0:T(8,128)}), s32[128,8,128]{2,1,0:T(8,128)S(1)}, u32[]{:S(2)}, u32[]{:S(2)}) async-start(s32[128,8,128]{2,1,0:T(8,128)} %constant_dynamic-slice_fusion), calls=%async_computation.2 | async-start | bytes 1048576 | tf_op jit(solution)/shard_map/all_to_all | solution.py:61
  85.7 9.9 %all-to-all-done.2 = s32[128,8,128]{2,1,0:T(8,128)S(1)} async-done(((s32[128,8,128]{2,1,0:T(8,128)}), s32[128,8,128]{2,1,0:T(8,128)S(1)}, u32[]{:S(2)}, u32[]{:S(2)}) %all-to-all-start.2) | async-done | bytes 524320 | tf_op jit(solution)/shard_map/all_to_all | solution.py:61
  95.6 4.3 %all-to-all-start.3 = ((f32[128,8,128]{2,1,0:T(8,128)}), f32[128,8,128]{2,1,0:T(8,128)S(1)}, u32[]{:S(2)}, u32[]{:S(2)}) async-start(f32[128,8,128]{2,1,0:T(8,128)} %reduce-scatter.2.cloned.1.call-done), calls=%async_computation.4 | async-start | bytes 1048576 | tf_op jit(solution)/shard_map/all_to_all | solution.py:56
  101.2 0.8 gather_fusion.4
  102.2 13.0 %all-to-all-done.3 = f32[128,8,128]{2,1,0:T(8,128)S(1)} async-done(((f32[128,8,128]{2,1,0:T(8,128)}), f32[128,8,128]{2,1,0:T(8,128)S(1)}, u32[]{:S(2)}, u32[]{:S(2)}) %all-to-all-start.3) | async-done | bytes 524320 | tf_op jit(solution)/shard_map/all_to_all | solution.py:56
  115.2 0.8 gather_fusion.6
  116.2 57.8 %while.11 = (s32[]{:T(128)}, f32[8,16,128,256]{3,2,1,0:T(8,128)}, s32[8,16,8,128]{3,2,1,0:T(8,128)S(1)}, f32[8,16,8,128]{3,2,1,0:T(8,128)S(1)}, s32[]{:T(128)}) while((s32[]{:T(128)}, f32[8,16,128,256]{3,2,1,0:T(8,128)}, s32[8,16,8,128]{3,2,1,0:T(8,128)S(1)}, f32[8,16,8,128]{3,2,1,0:T(8,128)S(1)}, s32[]{:T(128)}) %tuple.23), condition=%wide.region_10.11_spmd.clone, body=%wide.region_8.10_spmd.clone.sunk | while | flops 12058626 | bytes 6685253 | solution.py:23
  116.2 5.7 %select_reduce_fusion.4 = f32[16,128,256]{2,1,0:T(8,128)S(1)} fusion(f32[16,8,128]{2,1,0:T(8,128)S(1)} %dynamic-slice_bitcast_fusion.4, s32[16,8,128]{2,1,0:T(8,128)S(1)} %dynamic-slice_bitcast_fusion.5), kind=kLoop, calls=%fused_computation.16.clone.1 | loop fusion | flops 12058624 | bytes 2228224 | tf_op jit(solution)/shard_map/while/body/eval_jaxpr/reduce_sum | solution.py:21
  121.9 1.6 bitcast_dynamic-update-slice_fusion.2
  123.5 5.7 %select_reduce_fusion.4 = f32[16,128,256]{2,1,0:T(8,128)S(1)} fusion(f32[16,8,128]{2,1,0:T(8,128)S(1)} %dynamic-slice_bitcast_fusion.4, s32[16,8,128]{2,1,0:T(8,128)S(1)} %dynamic-slice_bitcast_fusion.5), kind=kLoop, calls=%fused_computation.16.clone.1 | loop fusion | flops 12058624 | bytes 2228224 | tf_op jit(solution)/shard_map/while/body/eval_jaxpr/reduce_sum | solution.py:21
  129.1 1.5 bitcast_dynamic-update-slice_fusion.2
  130.6 5.7 %select_reduce_fusion.4 = f32[16,128,256]{2,1,0:T(8,128)S(1)} fusion(f32[16,8,128]{2,1,0:T(8,128)S(1)} %dynamic-slice_bitcast_fusion.4, s32[16,8,128]{2,1,0:T(8,128)S(1)} %dynamic-slice_bitcast_fusion.5), kind=kLoop, calls=%fused_computation.16.clone.1 | loop fusion | flops 12058624 | bytes 2228224 | tf_op jit(solution)/shard_map/while/body/eval_jaxpr/reduce_sum | solution.py:21
  136.3 1.5 bitcast_dynamic-update-slice_fusion.2
  137.9 5.7 %select_reduce_fusion.4 = f32[16,128,256]{2,1,0:T(8,128)S(1)} fusion(f32[16,8,128]{2,1,0:T(8,128)S(1)} %dynamic-slice_bitcast_fusion.4, s32[16,8,128]{2,1,0:T(8,128)S(1)} %dynamic-slice_bitcast_fusion.5), kind=kLoop, calls=%fused_computation.16.clone.1 | loop fusion | flops 12058624 | bytes 2228224 | tf_op jit(solution)/shard_map/while/body/eval_jaxpr/reduce_sum | solution.py:21
  143.5 1.5 bitcast_dynamic-update-slice_fusion.2
  145.1 5.7 %select_reduce_fusion.4 = f32[16,128,256]{2,1,0:T(8,128)S(1)} fusion(f32[16,8,128]{2,1,0:T(8,128)S(1)} %dynamic-slice_bitcast_fusion.4, s32[16,8,128]{2,1,0:T(8,128)S(1)} %dynamic-slice_bitcast_fusion.5), kind=kLoop, calls=%fused_computation.16.clone.1 | loop fusion | flops 12058624 | bytes 2228224 | tf_op jit(solution)/shard_map/while/body/eval_jaxpr/reduce_sum | solution.py:21
  150.8 1.6 bitcast_dynamic-update-slice_fusion.2
  152.4 5.7 %select_reduce_fusion.4 = f32[16,128,256]{2,1,0:T(8,128)S(1)} fusion(f32[16,8,128]{2,1,0:T(8,128)S(1)} %dynamic-slice_bitcast_fusion.4, s32[16,8,128]{2,1,0:T(8,128)S(1)} %dynamic-slice_bitcast_fusion.5), kind=kLoop, calls=%fused_computation.16.clone.1 | loop fusion | flops 12058624 | bytes 2228224 | tf_op jit(solution)/shard_map/while/body/eval_jaxpr/reduce_sum | solution.py:21
  158.0 1.5 bitcast_dynamic-update-slice_fusion.2
  159.5 5.7 %select_reduce_fusion.4 = f32[16,128,256]{2,1,0:T(8,128)S(1)} fusion(f32[16,8,128]{2,1,0:T(8,128)S(1)} %dynamic-slice_bitcast_fusion.4, s32[16,8,128]{2,1,0:T(8,128)S(1)} %dynamic-slice_bitcast_fusion.5), kind=kLoop, calls=%fused_computation.16.clone.1 | loop fusion | flops 12058624 | bytes 2228224 | tf_op jit(solution)/shard_map/while/body/eval_jaxpr/reduce_sum | solution.py:21
  165.2 1.6 bitcast_dynamic-update-slice_fusion.2
  166.8 5.7 %select_reduce_fusion.4 = f32[16,128,256]{2,1,0:T(8,128)S(1)} fusion(f32[16,8,128]{2,1,0:T(8,128)S(1)} %dynamic-slice_bitcast_fusion.4, s32[16,8,128]{2,1,0:T(8,128)S(1)} %dynamic-slice_bitcast_fusion.5), kind=kLoop, calls=%fused_computation.16.clone.1 | loop fusion | flops 12058624 | bytes 2228224 | tf_op jit(solution)/shard_map/while/body/eval_jaxpr/reduce_sum | solution.py:21
  172.5 1.5 bitcast_dynamic-update-slice_fusion.2
  174.0 8.0 %multiply_reduce_fusion.2 = f32[8,16,128]{2,1,0:T(8,128)S(1)} fusion(f32[8,16,128,256]{3,2,1,0:T(8,128)} %get-tuple-element.32, f32[8,16,256]{2,1,0:T(8,128)S(1)} %bitcast.73), kind=kLoop, calls=%fused_computation.22 | loop fusion | flops 8372224 | bytes 16973824 | tf_op jit(solution)/shard_map/reduce_sum | solution.py:80
  182.0 9.1 %all_gather.19 = f32[4,128,128]{2,1,0:T(8,128)S(1)} all-gather(f32[1,128,128]{2,1,0:T(8,128)S(1)} %bitcast.75), channel_id=1, replica_groups=mesh['src'=4,'blk'=8] {'src'}, dimensions={0}, use_global_device_ids=true | all-gather | bytes 327680 | tf_op jit(solution)/shard_map/all_gather | solution.py:81
  192.0 8.0 %multiply_reduce_fusion.1 = f32[8,16,128]{2,1,0:T(8,128)S(1)} fusion(f32[8,16,128,256]{3,2,1,0:T(8,128)} %get-tuple-element.32, f32[8,16,256]{2,1,0:T(8,128)S(1)} %pad_maximum_fusion), kind=kLoop, calls=%fused_computation.21 | loop fusion | flops 8372224 | bytes 16973824 | tf_op jit(solution)/shard_map/reduce_sum | solution.py:80
  200.0 8.1 %all_gather.21 = f32[4,128,128]{2,1,0:T(8,128)S(1)} all-gather(f32[1,128,128]{2,1,0:T(8,128)S(1)} %bitcast.76), channel_id=1, replica_groups=mesh['src'=4,'blk'=8] {'src'}, dimensions={0}, use_global_device_ids=true | all-gather | bytes 327680 | tf_op jit(solution)/shard_map/all_gather | solution.py:81
  209.0 8.0 %multiply_reduce_fusion = f32[8,16,128]{2,1,0:T(8,128)S(1)} fusion(f32[8,16,128,256]{3,2,1,0:T(8,128)} %get-tuple-element.32, f32[8,16,256]{2,1,0:T(8,128)S(1)} %pad_maximum_fusion.1), kind=kLoop, calls=%fused_computation.20 | loop fusion | flops 8372224 | bytes 16973824 | tf_op jit(solution)/shard_map/reduce_sum | solution.py:80
  217.0 9.1 %all_gather.23 = f32[4,128,128]{2,1,0:T(8,128)S(1)} all-gather(f32[1,128,128]{2,1,0:T(8,128)S(1)} %bitcast.74), channel_id=1, replica_groups=mesh['src'=4,'blk'=8] {'src'}, dimensions={0}, use_global_device_ids=true | all-gather | bytes 327680 | tf_op jit(solution)/shard_map/all_gather | solution.py:81
  226.8 0.7 broadcast_select_fusion.2
  227.5 3.3 %all-to-all-start.5 = ((f32[8,16,128]{2,1,0:T(8,128)}), f32[8,16,128]{2,1,0:T(8,128)S(1)}, u32[]{:S(2)}, u32[]{:S(2)}) async-start(f32[8,16,128]{2,1,0:T(8,128)} %broadcast_select_fusion.2), calls=%async_computation.6 | async-start | bytes 131072 | tf_op jit(solution)/shard_map/all_to_all | solution.py:84
  230.9 5.8 %all-to-all-done.5 = f32[8,16,128]{2,1,0:T(8,128)S(1)} async-done(((f32[8,16,128]{2,1,0:T(8,128)}), f32[8,16,128]{2,1,0:T(8,128)S(1)}, u32[]{:S(2)}, u32[]{:S(2)}) %all-to-all-start.5) | async-done | bytes 65568 | tf_op jit(solution)/shard_map/all_to_all | solution.py:84
  236.7 1.2 gather_fusion.13
  (71 shorter events, 10.0 us)
Async XLA Ops:
  6.5 5.5 %copy-start = (f32[1,64,32,128]{3,2,1,0:T(8,128)S(1)}, f32[1,64,32,128]{3,2,1,0:T(8,128)}, u32[]{:S(2)}) copy-start(f32[1,64,32,128]{3,2,1,0:T(8,128)} %param.9) | copy-start | bytes 3145732
  6.5 50.6 %all-reduce.4.cloned.1.call-start = ((), (), s32[]{:S(2)}) async-start(), calls=%async_computation.8 | async-start | bytes 262144 | tf_op jit(solution)/shard_map/psum | solution.py:53
  11.9 83.6 %reduce-scatter.2.cloned.1.call-start = ((), (), s32[]{:S(2)}) async-start(), calls=%async_computation.7 | async-start | bytes 2621440 | tf_op jit(solution)/shard_map/reduce_scatter | solution.py:52
  57.1 10.5 %all-to-all-start.1 = ((f32[8,16,128]{2,1,0:T(8,128)}), f32[8,16,128]{2,1,0:T(8,128)S(1)}, u32[]{:S(2)}, u32[]{:S(2)}) async-start(f32[8,16,128]{2,1,0:T(8,128)} %get-tuple-element.52), calls=%async_computation.1 | async-start | bytes 131072 | tf_op jit(solution)/shard_map/all_to_all | solution.py:58
  67.6 9.2 %all-to-all-start.4 = ((f32[8,16,128]{2,1,0:T(8,128)}), f32[8,16,128]{2,1,0:T(8,128)S(1)}, u32[]{:S(2)}, u32[]{:S(2)}) async-start(f32[8,16,128]{2,1,0:T(8,128)} %get-tuple-element.51), calls=%async_computation.5 | async-start | bytes 131072 | tf_op jit(solution)/shard_map/all_to_all | solution.py:57
  76.8 18.8 %all-to-all-start.2 = ((s32[128,8,128]{2,1,0:T(8,128)}), s32[128,8,128]{2,1,0:T(8,128)S(1)}, u32[]{:S(2)}, u32[]{:S(2)}) async-start(s32[128,8,128]{2,1,0:T(8,128)} %constant_dynamic-slice_fusion), calls=%async_computation.2 | async-start | bytes 1048576 | tf_op jit(solution)/shard_map/all_to_all | solution.py:61
  95.6 19.6 %all-to-all-start.3 = ((f32[128,8,128]{2,1,0:T(8,128)}), f32[128,8,128]{2,1,0:T(8,128)S(1)}, u32[]{:S(2)}, u32[]{:S(2)}) async-start(f32[128,8,128]{2,1,0:T(8,128)} %reduce-scatter.2.cloned.1.call-done), calls=%async_computation.4 | async-start | bytes 1048576 | tf_op jit(solution)/shard_map/all_to_all | solution.py:56
  192.0 38.9 %copy-start.1 = (s32[64,1]{0,1:T(1,128)S(1)}, s32[64,1]{0,1:T(1,128)}, u32[]{:S(2)}) copy-start(s32[64,1]{0,1:T(1,128)} %param.14) | copy-start | bytes 772
  227.5 9.2 %all-to-all-start.5 = ((f32[8,16,128]{2,1,0:T(8,128)}), f32[8,16,128]{2,1,0:T(8,128)S(1)}, u32[]{:S(2)}, u32[]{:S(2)}) async-start(f32[8,16,128]{2,1,0:T(8,128)} %broadcast_select_fusion.2), calls=%async_computation.6 | async-start | bytes 131072 | tf_op jit(solution)/shard_map/all_to_all | solution.py:84
Sparse Core Ops, SparseCore 0:
  12.1 44.9 all-reduce.3
  60.1 35.1 reduce-scatter.1
